TPU v7x, 32 devices: a whole 2x2x4 slice. The times are simulated.
32 devices in a mesh: dp: 8 (over y, x, core), tensor: 4 (over z).
Axes of the slice: x: 2, y: 2, z: 4, core: 2. Of those that a mesh axis runs over, the one named last changes fastest.
Arguments:
- images: bfloat16 [32, 320, 1024], P('dp', None, 'tensor'), may hold values from -6 to 6
- lengths: int32 [32], P('dp'), may hold values from 224 to 320, as said below
- cotangent: bfloat16 [32, 320, 1024], P('dp', None, 'tensor'), may hold values from -6 to 6
- norm1_gain: float32 [1024], replicated, may hold values from 0.5 to 1.5
- norm1_shift: float32 [1024], replicated, may hold values from -1.75 to 1.75
- w_qkv: bfloat16 [1024, 3, 1024], P(None, None, 'tensor'), may hold values from -0.1875 to 0.1875
- qv_bias: float32 [2, 1024], P(None, 'tensor'), may hold values from -3 to 3
- w_proj: bfloat16 [1024, 1024], P('tensor'), may hold values from -1.5 to 1.5
- proj_bias: float32 [1024], replicated, may hold values from -3 to 3
- norm2_gain: float32 [1024], replicated, may hold values from 0.5 to 1.5
- norm2_shift: float32 [1024], replicated, may hold values from -1.75 to 1.75
- w_fc1: bfloat16 [1024, 4096], P(None, 'tensor'), may hold values from -0.1875 to 0.1875
- fc1_bias: float32 [4096], P('tensor'), may hold values from -3 to 3
- w_fc2: bfloat16 [4096, 1024], P('tensor'), may hold values from -0.09375 to 0.09375
- fc2_bias: float32 [1024], replicated, may hold values from -3 to 3
Outputs:
- output: bfloat16 [32, 320, 1024], P('dp', None, 'tensor')
- input_grad: bfloat16 [32, 320, 1024], P('dp', None, 'tensor')
- grad_norm1_gain: float32 [1024], replicated
- grad_norm1_shift: float32 [1024], replicated
- grad_w_qkv: float32 [1024, 3, 1024], P(None, None, 'tensor')
- grad_qv_bias: float32 [2, 1024], P(None, 'tensor')
- grad_w_proj: float32 [1024, 1024], P('tensor')
- grad_proj_bias: float32 [1024], replicated
- grad_norm2_gain: float32 [1024], replicated
- grad_norm2_shift: float32 [1024], replicated
- grad_w_fc1: float32 [1024, 4096], P(None, 'tensor')
- grad_fc1_bias: float32 [4096], P('tensor')
- grad_w_fc2: float32 [4096, 1024], P('tensor')
- grad_fc2_bias: float32 [1024], replicated
Inputs may be any that keep to these rules, and one draw needn't show every extreme that they name: lengths[i] is the number of valid slots of image i, which come first; some image has all 320 slots valid in every draw.
All inputs are finite; a program needn't handle non-finite values.
Results may differ from a plain program's by a relative error of at most 0.02.
Values may be sent and summed in bfloat16 or wider, within the bound.
A program may use at most 192 MiB of HBM per device.

v0:
```python
import jax
import jax.numpy as jnp
from jax import lax
from jax.sharding import PartitionSpec as P

HEAD_DIM = 64
EPS = 1e-06
MASKED = -1e30


def norm_rows(values, gain_row, shift_row):
    row_mean = jnp.mean(values, axis=-1, keepdims=True)
    centered = values - row_mean
    spread = jnp.mean(centered * centered, axis=-1, keepdims=True)
    inverse = lax.rsqrt(spread + EPS)
    unit_rows = centered * inverse
    return (unit_rows * gain_row + shift_row, unit_rows, inverse)


def norm_back(gradient, unit_rows, inverse, gain_row):
    scaled = gradient * gain_row
    first_mean = jnp.mean(scaled, axis=-1, keepdims=True)
    cross_mean = jnp.mean(scaled * unit_rows, axis=-1, keepdims=True)
    return inverse * (scaled - first_mean - unit_rows * cross_mean)


def scores_of(queries, key_heads, key_mask, score_scale):
    raw_scores = (
        jnp.einsum("bqhe,bkhe->bhqk", queries, key_heads, preferred_element_type=jnp.float32)
        * score_scale
    )
    return jnp.where(key_mask, raw_scores, MASKED)


def exact_gelu(values):
    return jax.nn.gelu(values, approximate=False)


def per_device(
    images,
    lengths,
    cotangent,
    norm1_gain,
    norm1_shift,
    w_qkv,
    qv_bias,
    w_proj,
    proj_bias,
    norm2_gain,
    norm2_shift,
    w_fc1,
    fc1_bias,
    w_fc2,
    fc2_bias,
):
    images_here, slot_count, col_count = images.shape
    model_width = w_qkv.shape[0]
    local_width = w_qkv.shape[2]
    heads_here = local_width // HEAD_DIM
    row_count = images_here * slot_count
    score_scale = HEAD_DIM ** (-0.5)
    first_col = lax.axis_index("tensor") * col_count
    full_images, full_cot = (
        lax.all_gather(images, "tensor", axis=2, tiled=True),
        lax.all_gather(cotangent, "tensor", axis=2, tiled=True),
    )
    slot_ids = jnp.arange(slot_count, dtype=jnp.int32)
    valid_slots = (slot_ids[None, :] < lengths[:, None]).astype(jnp.float32)
    keep_rows = valid_slots.reshape(row_count, 1)
    row_values = full_images.reshape(row_count, model_width).astype(jnp.float32) * keep_rows
    normed1, unit1, inverse1 = norm_rows(row_values, norm1_gain, norm1_shift)
    normed1 = normed1.astype(jnp.bfloat16)
    qkv_bias = jnp.concatenate([qv_bias[0], jnp.zeros_like(qv_bias[0]), qv_bias[1]])
    w_flat = w_qkv.reshape(model_width, 3 * local_width)
    qkv_rows = (jnp.dot(normed1, w_flat, preferred_element_type=jnp.float32) + qkv_bias).astype(
        jnp.bfloat16
    )
    qkv_rows = qkv_rows.reshape(images_here, slot_count, 3, heads_here, HEAD_DIM)
    queries = qkv_rows[:, :, 0]
    key_heads = qkv_rows[:, :, 1]
    value_heads = qkv_rows[:, :, 2]
    key_mask = valid_slots[:, None, None, :] > 0
    scores = scores_of(queries, key_heads, key_mask, score_scale)
    row_top = jnp.max(scores, axis=-1, keepdims=True)
    shifted = jnp.exp(scores - row_top)
    row_total = jnp.sum(shifted, axis=-1, keepdims=True)
    probability = (shifted / row_total).astype(jnp.bfloat16)
    log_total = row_top + jnp.log(row_total)
    mixed = jnp.einsum(
        "bhqk,bkhe->bqhe", probability, value_heads, preferred_element_type=jnp.float32
    ).astype(jnp.bfloat16)
    mixed_rows = mixed.reshape(row_count, local_width)
    attn_part = jnp.dot(mixed_rows, w_proj, preferred_element_type=jnp.float32)
    middle = (
        row_values
        + lax.psum(attn_part.astype(jnp.bfloat16), "tensor").astype(jnp.float32)
        + proj_bias
    )
    normed2, unit2, inverse2 = norm_rows(middle, norm2_gain, norm2_shift)
    normed2 = normed2.astype(jnp.bfloat16)
    pre_act = jnp.dot(normed2, w_fc1, preferred_element_type=jnp.float32) + fc1_bias
    activated = exact_gelu(pre_act).astype(jnp.bfloat16)
    ff_part = jnp.dot(activated, w_fc2, preferred_element_type=jnp.float32)
    ff_share = lax.psum_scatter(
        ff_part.astype(jnp.bfloat16), "tensor", scatter_dimension=1, tiled=True
    ).astype(jnp.float32)
    middle_cols = lax.dynamic_slice_in_dim(middle, first_col, col_count, 1)
    bias_cols = lax.dynamic_slice_in_dim(fc2_bias, first_col, col_count, 0)
    output = ((middle_cols + ff_share + bias_cols) * keep_rows).astype(jnp.bfloat16)
    output = output.reshape(images_here, slot_count, col_count)
    grad_out = full_cot.reshape(row_count, model_width).astype(jnp.float32) * keep_rows
    grad_ff = grad_out.astype(jnp.bfloat16)
    grad_fc2_bias = jnp.sum(grad_ff, axis=0, dtype=jnp.float32)
    grad_w_fc2 = jnp.einsum("rf,rd->fd", activated, grad_ff, preferred_element_type=jnp.float32)
    grad_act = jnp.einsum("rd,fd->rf", grad_ff, w_fc2, preferred_element_type=jnp.float32)
    gelu_pull = jax.vjp(exact_gelu, pre_act)[1]
    grad_pre = gelu_pull(grad_act)[0].astype(jnp.bfloat16)
    grad_fc1_bias = jnp.sum(grad_pre, axis=0, dtype=jnp.float32)
    grad_w_fc1 = jnp.einsum("rd,rf->df", normed2, grad_pre, preferred_element_type=jnp.float32)
    hidden_part = jnp.einsum("rf,df->rd", grad_pre, w_fc1, preferred_element_type=jnp.float32)
    grad_normed2 = lax.psum(hidden_part.astype(jnp.bfloat16), "tensor").astype(jnp.float32)
    grad_norm2_gain = jnp.sum(grad_normed2 * unit2, axis=0)
    grad_norm2_shift = jnp.sum(grad_normed2, axis=0)
    grad_middle = grad_out + norm_back(grad_normed2, unit2, inverse2, norm2_gain)
    grad_attn = grad_middle.astype(jnp.bfloat16)
    grad_proj_bias = jnp.sum(grad_attn, axis=0, dtype=jnp.float32)
    grad_w_proj = jnp.einsum("rc,rd->cd", mixed_rows, grad_attn, preferred_element_type=jnp.float32)
    grad_mixed = jnp.einsum(
        "rd,cd->rc", grad_attn, w_proj, preferred_element_type=jnp.float32
    ).astype(jnp.bfloat16)
    grad_mixed = grad_mixed.reshape(images_here, slot_count, heads_here, HEAD_DIM)
    scores_again = scores_of(queries, key_heads, key_mask, score_scale)
    weights_soft = jnp.exp(scores_again - log_total)
    grad_value = jnp.einsum(
        "bhqk,bqhe->bkhe",
        weights_soft.astype(jnp.bfloat16),
        grad_mixed,
        preferred_element_type=jnp.float32,
    )
    grad_prob = jnp.einsum(
        "bqhe,bkhe->bhqk", grad_mixed, value_heads, preferred_element_type=jnp.float32
    )
    row_dot = jnp.sum(weights_soft * grad_prob, axis=-1, keepdims=True)
    grad_scores = (weights_soft * (grad_prob - row_dot)).astype(jnp.bfloat16)
    grad_query = (
        jnp.einsum("bhqk,bkhe->bqhe", grad_scores, key_heads, preferred_element_type=jnp.float32)
        * score_scale
    )
    grad_key = (
        jnp.einsum("bhqk,bqhe->bkhe", grad_scores, queries, preferred_element_type=jnp.float32)
        * score_scale
    )
    grad_qkv = jnp.stack([grad_query, grad_key, grad_value], axis=2).astype(jnp.bfloat16)
    grad_qkv = grad_qkv.reshape(row_count, 3 * local_width)
    bias_sums = jnp.sum(grad_qkv, axis=0, dtype=jnp.float32).reshape(3, local_width)
    grad_qv_bias = jnp.stack([bias_sums[0], bias_sums[2]])
    grad_w_qkv = jnp.einsum("rd,rc->dc", normed1, grad_qkv, preferred_element_type=jnp.float32)
    grad_w_qkv = grad_w_qkv.reshape(model_width, 3, local_width)
    normed_part = jnp.einsum("rc,dc->rd", grad_qkv, w_flat, preferred_element_type=jnp.float32)
    grad_normed1 = lax.psum(normed_part.astype(jnp.bfloat16), "tensor").astype(jnp.float32)
    grad_norm1_gain = jnp.sum(grad_normed1 * unit1, axis=0)
    grad_norm1_shift = jnp.sum(grad_normed1, axis=0)
    grad_full = grad_middle + norm_back(grad_normed1, unit1, inverse1, norm1_gain)
    grad_input = lax.dynamic_slice_in_dim(grad_full, first_col, col_count, 1) * keep_rows
    input_grad = grad_input.astype(jnp.bfloat16).reshape(images_here, slot_count, col_count)
    summed = (
        lax.psum(grad_norm1_gain.astype(jnp.bfloat16), "dp").astype(jnp.float32),
        lax.psum(grad_norm1_shift.astype(jnp.bfloat16), "dp").astype(jnp.float32),
        lax.psum(grad_w_qkv.astype(jnp.bfloat16), "dp").astype(jnp.float32),
        lax.psum(grad_qv_bias.astype(jnp.bfloat16), "dp").astype(jnp.float32),
        lax.psum(grad_w_proj.astype(jnp.bfloat16), "dp").astype(jnp.float32),
        lax.psum(grad_proj_bias.astype(jnp.bfloat16), "dp").astype(jnp.float32),
        lax.psum(grad_norm2_gain.astype(jnp.bfloat16), "dp").astype(jnp.float32),
        lax.psum(grad_norm2_shift.astype(jnp.bfloat16), "dp").astype(jnp.float32),
        lax.psum(grad_w_fc1.astype(jnp.bfloat16), "dp").astype(jnp.float32),
        lax.psum(grad_fc1_bias.astype(jnp.bfloat16), "dp").astype(jnp.float32),
        lax.psum(grad_w_fc2.astype(jnp.bfloat16), "dp").astype(jnp.float32),
        lax.psum(grad_fc2_bias.astype(jnp.bfloat16), "dp").astype(jnp.float32),
    )
    return (
        output,
        input_grad,
        summed[0],
        summed[1],
        summed[2],
        summed[3],
        summed[4],
        summed[5],
        summed[6],
        summed[7],
        summed[8],
        summed[9],
        summed[10],
        summed[11],
    )


def solution(mesh):
    in_specs = (
        P("dp", None, "tensor"),
        P("dp"),
        P("dp", None, "tensor"),
        P(),
        P(),
        P(None, None, "tensor"),
        P(None, "tensor"),
        P("tensor", None),
        P(),
        P(),
        P(),
        P(None, "tensor"),
        P("tensor"),
        P("tensor", None),
        P(),
    )
    out_specs = (
        P("dp", None, "tensor"),
        P("dp", None, "tensor"),
        P(),
        P(),
        P(None, None, "tensor"),
        P(None, "tensor"),
        P("tensor", None),
        P(),
        P(),
        P(),
        P(None, "tensor"),
        P("tensor"),
        P("tensor", None),
        P(),
    )
    return jax.shard_map(
        per_device, mesh=mesh, in_specs=in_specs, out_specs=out_specs, check_vma=False
    )
```

profile of v0, /device:TPU:0, one launch (start us, length us, event | category | flops | bytes accessed | tf_op | source)
XLA Modules:
  0.0 699.4 jit_solution(9213317824829638723)
XLA Ops:
  10.2 2.6 copy.39
  12.8 54.3 %all-gather.3.cloned.1.call-done = bf16[4,320,1024]{2,1,0:T(8,128)(2,1)} async-done(((bf16[4,320,256]{2,1,0:T(8,128)(2,1)}), bf16[4,320,1024]{2,1,0:T(8,128)(2,1)}) %all-gather.3.cloned.1.call-update) | async-done | bytes 2621456 | tf_op jit(solution)/shard_map/all_gather | solution.py:64
  67.2 2.6 fusion.18
  69.8 2.8 multiply_reduce_fusion.3
  75.4 3.5 add_convert_fusion.3
  78.9 6.7 reshape.265
  85.6 4.0 fusion.57
  89.6 2.3 copy.64
  91.8 2.5 copy.65
  94.3 3.2 copy.66
  97.5 3.2 fusion.24
  102.7 2.4 fusion.35
  108.7 3.4 convolution_convert_fusion.1
  112.3 9.5 %all-gather.5.cloned.1.call-done = bf16[4,320,1024]{2,1,0:T(8,128)(2,1)} async-done(((bf16[4,320,256]{2,1,0:T(8,128)(2,1)}), bf16[4,320,1024]{2,1,0:T(8,128)(2,1)}) %all-gather.5.cloned.1.call-update) | async-done | bytes 2621456 | tf_op jit(solution)/shard_map/all_gather | solution.py:65
  121.8 105.2 %all-reduce.7.cloned.1.call-done = bf16[1280,1024]{1,0:T(8,128)(2,1)} async-done(((bf16[1280,1024]{1,0:T(8,128)(2,1)}), bf16[1280,1024]{1,0:T(8,128)(2,1)}) %all-reduce.7.cloned.1.call-update) | async-done | bytes 2621456 | tf_op jit(solution)/shard_map/psum | solution.py:96
  227.0 5.0 fusion.56
  232.8 2.5 copy-done.48
  235.3 3.0 fusion.51
  238.4 16.8 %fusion.52 = (bf16[1024]{0:T(1024)(128)(2,1)}, bf16[1280,1024]{1,0:T(8,128)(2,1)S(1)}, f32[1280,1024]{1,0:T(8,128)}) fusion(f32[1280,1024]{1,0:T(8,128)S(1)} %fusion.51, f32[1024]{0:T(1024)S(1)} %copy-done.45, bf16[1280,1024]{1,0:T(8,128)(2,1)S(1)} %get-tuple-element.49, bf16[1024,1024]{1,0:T(8,128)(2,1)S(1)} %copy-done), kind=kOutput, calls=%fused_computation.113 | convolution fusion | flops 2781346816 | bytes 17831936 | tf_op jit(solution)/shard_map/rd,fd->rf/dot_general | solution.py:115
  256.6 4.2 convolution_convert_fusion.2
  262.3 101.8 %all-reduce.9.cloned.1.call-done = bf16[1280,1024]{1,0:T(8,128)(2,1)} async-done(((bf16[1280,1024]{1,0:T(8,128)(2,1)}), bf16[1280,1024]{1,0:T(8,128)(2,1)}) %all-reduce.9.cloned.1.call-update) | async-done | bytes 2621456 | tf_op jit(solution)/shard_map/psum | solution.py:121
  364.1 5.5 fusion.9
  369.6 5.6 convert_reduce_fusion
  375.2 2.3 copy-done.4
  379.2 3.1 reshape.266
  382.3 3.2 copy.47
  385.5 5.5 fusion.27
  391.1 5.4 multiply_reduce_fusion
  396.5 2.9 multiply_convert_fusion
  402.2 3.2 copy.52
  405.5 4.7 convert_element_type.226
  410.2 5.7 convolution_convert_fusion
  416.0 5.5 multiply_convert_fusion.2
  423.0 4.1 convolution_convert_fusion.3
  427.4 7.1 %convolution_convert_fusion.5 = bf16[1024,1024]{1,0:T(8,128)(2,1)} fusion(bf16[1280,1024]{1,0:T(8,128)(2,1)} %copy-done.15, bf16[1280,1024]{1,0:T(8,128)(2,1)} %copy-done.12), kind=kOutput, calls=%fused_computation.66 | convolution fusion | flops 2685403136 | bytes 7340032 | tf_op jit(solution)/shard_map/rf,rd->fd/dot_general | solution.py:114
  434.5 7.3 %convolution_convert_fusion.6 = bf16[1024,1024]{1,0:T(8,128)(2,1)} fusion(bf16[1280,1024]{1,0:T(8,128)(2,1)S(1)} %copy-done.52, f32[1280,1024]{1,0:T(8,128)} %copy-done.2, f32[1024]{0:T(1024)S(1)} %copy-done.50, f32[1024]{0:T(1024)S(1)} %copy-done.38, f32[1280]{0:T(1024)S(1)} %copy-done.31, f32[1280]{0:T(1024)S(1)} %copy-done.25), kind=kOutput, calls=%fused_computation.67 | convolution fusion | flops 2691956736 | bytes 9979904 | tf_op jit(solution)/shard_map/rd,rf->df/dot_general | solution.py:119
  444.4 3.4 convolution_convert_fusion.7
  448.8 2.3 fusion.25
  451.3 67.9 %all-reduce.11.cloned.1.call-done = bf16[1280,1024]{1,0:T(8,128)(2,1)} async-done(((bf16[1280,1024]{1,0:T(8,128)(2,1)}), bf16[1280,1024]{1,0:T(8,128)(2,1)}) %all-reduce.11.cloned.1.call-update) | async-done | bytes 2621456 | tf_op jit(solution)/shard_map/psum | solution.py:160
  521.4 7.4 %fusion.10 = (bf16[1024]{0:T(1024)(128)(2,1)S(1)}, f32[1280]{0:T(1024)S(1)}, f32[1280]{0:T(1024)S(1)}, f32[1280,1024]{1,0:T(8,128)}, f32[1280,1024]{1,0:T(8,128)}) fusion(bf16[1280,1024]{1,0:T(8,128)(2,1)} %all-reduce.11.cloned.1.call-done, f32[1280]{0:T(1024)S(1)} %rsqrt.22, f32[1280]{0:T(1024)S(1)} %div.43, f32[1280]{0:T(1024)S(1)} %reshape.262, ...), kind=kLoop, calls=%fused_computation.21 | loop fusion | flops 14414336 | bytes 15760384 | tf_op jit(solution)/shard_map/reduce_sum | solution.py:161
  528.9 24.7 %all-reduce = (bf16[1024]{0:T(1024)(128)(2,1)S(1)}, bf16[1024]{0:T(1024)(128)(2,1)S(1)}, bf16[2,256]{1,0:T(2,128)(2,1)S(1)}, bf16[1024]{0:T(1024)(128)(2,1)S(1)}...) all-reduce(bf16[1024]{0:T(1024)(128)(2,1)S(1)} %get-tuple-element.1, ...), channel_id=1, replica_groups=mesh['dp'=8,'tensor'=4] {'dp'}, use_global_device_ids=true, to_apply=%region_16.17 | all-reduce | flops 7680 | bytes 30720 | tf_op jit(solution)/shard_map/psum | solution.py:167
  558.3 14.9 %reduce-scatter.2.cloned.1.call-done = bf16[1280,256]{1,0:T(8,128)(2,1)} async-done(((bf16[1280,1024]{1,0:T(8,128)(2,1)}), bf16[1280,256]{1,0:T(8,128)(2,1)}) %reduce-scatter.2.cloned.1.call-update) | async-done | bytes 655376 | tf_op jit(solution)/shard_map/reduce_scatter | solution.py:104
  573.2 4.1 fusion.32
  577.3 104.3 %all-reduce.13.cloned.1.call-done = (bf16[1024,3,256]{2,0,1:T(8,128)(2,1)}, bf16[256,1024]{1,0:T(8,128)(2,1)}, bf16[1024,1024]{1,0:T(8,128)(2,1)}, bf16[1024,1024]{1,0:T(8,128)(2,1)}) async-done(((bf16[1024,3,256]{2,0,1:T(8,128)(2,1)}, bf16[256,1024]{1,0:T(8,128)(2,1)}, bf16[1024,1024]{1,0:T(8,128)(2,1)}, bf16[1024,1024]{1,0:T(8,128)(2,1)}), (bf16[1024,3,256]{2,0,1:T(8,128)(2,1)}, ...) | async-done | bytes 6291472 | tf_op jit(solution)/shard_map/psum | solution.py:169
  681.6 2.3 convert_element_type.238
  683.9 3.5 convert_element_type.234
  687.4 2.5 convert_element_type.244
  689.8 2.5 convert_element_type.247
  (167 shorter events, 32.1 us)
Async XLA Ops:
  7.2 231.2 %copy-start = (bf16[1024,1024]{1,0:T(8,128)(2,1)S(1)}, bf16[1024,1024]{1,0:T(8,128)(2,1)}, u32[]{:S(2)}) copy-start(bf16[1024,1024]{1,0:T(8,128)(2,1)} %param.28) | copy-start | bytes 6291460
  7.2 65.4 %copy-start.39 = (f32[1024]{0:T(1024)S(1)}, f32[1024]{0:T(1024)}, u32[]{:S(2)}) copy-start(f32[1024]{0:T(1024)} %param.18) | copy-start | bytes 12292
  7.2 65.3 %copy-start.44 = (f32[1024]{0:T(1024)S(1)}, f32[1024]{0:T(1024)}, u32[]{:S(2)}) copy-start(f32[1024]{0:T(1024)} %param.19) | copy-start | bytes 12292
  7.2 60.0 %all-gather.3.cloned.1.call-start = ((), (), s32[]{:S(2)}) async-start(), calls=%async_computation.1 | async-start | bytes 3276800 | tf_op jit(solution)/shard_map/all_gather | solution.py:64
  8.0 113.8 %all-gather.5.cloned.1.call-start = ((), (), s32[]{:S(2)}) async-start(), calls=%async_computation.4 | async-start | bytes 3276800 | tf_op jit(solution)/shard_map/all_gather | solution.py:65
  8.7 218.3 %all-reduce.7.cloned.1.call-start = ((), (), s32[]{:S(2)}) async-start(), calls=%async_computation.2 | async-start | bytes 5242880 | tf_op jit(solution)/shard_map/psum | solution.py:96
  10.2 92.5 %copy-start.34 = (pred[4,320]{1,0:T(4,128)(4,1)}, pred[4,320]{1,0:T(4,128)(4,1)S(1)}, u32[]{:S(2)}) copy-start(pred[4,320]{1,0:T(4,128)(4,1)S(1)} %get-tuple-element.54) | copy-start | bytes 3844
  67.2 5.4 copy-start.3
  67.2 8.2 %copy-start.20 = (bf16[1024,3,256]{0,2,1:T(8,128)(2,1)S(1)}, bf16[1024,3,256]{0,2,1:T(8,128)(2,1)}, u32[]{:S(2)}) copy-start(bf16[1024,3,256]{0,2,1:T(8,128)(2,1)} %copy.39) | copy-start | bytes 4718596
  69.7 4.1 copy-start.26
  100.7 4.4 copy-start.1
  100.8 4.4 copy-start.22
  112.2 251.9 %all-reduce.9.cloned.1.call-start = ((), (), s32[]{:S(2)}) async-start(), calls=%async_computation.5 | async-start | bytes 5242880 | tf_op jit(solution)/shard_map/psum | solution.py:121
  232.0 6.3 copy-start.2
  232.0 6.3 copy-start.12
  232.0 3.2 copy-start.48
  232.1 6.2 copy-start.23
  238.3 16.8 %copy-start.8 = (f32[1280,1024]{1,0:T(8,128)}, f32[1280,1024]{1,0:T(8,128)S(1)}, u32[]{:S(2)}) copy-start(f32[1280,1024]{1,0:T(8,128)S(1)} %fusion.51) | copy-start | bytes 15728644
  260.9 258.3 %all-reduce.11.cloned.1.call-start = ((), (), s32[]{:S(2)}) async-start(), calls=%async_computation.6 | async-start | bytes 5242880 | tf_op jit(solution)/shard_map/psum | solution.py:160
  364.1 5.5 copy-start.5
  364.1 5.5 copy-start.6
  364.1 5.5 copy-start.24
  364.1 5.5 copy-start.30
  364.1 5.5 copy-start.37
  369.6 7.8 %copy-start.18 = (bf16[256,1024]{1,0:T(8,128)(2,1)S(1)}, bf16[256,1024]{1,0:T(8,128)(2,1)}, u32[]{:S(2)}) copy-start(bf16[256,1024]{1,0:T(8,128)(2,1)} %param.22) | copy-start | bytes 1572868
  385.5 5.5 copy-start.10
  385.5 5.6 copy-start.11
  385.5 5.6 copy-start.21
  385.5 5.6 copy-start.35
  385.5 11.0 %slice-start = ((s8[7864320]{0:T(1024)(128)(4,1)}), s8[4194304]{0:T(1024)(128)(4,1)S(1)}, s32[]{:S(2)}) async-start(s8[7864320]{0:T(1024)(128)(4,1)} %bitcast.95), calls=%async_computation.8 | async-start | bytes 8388608
  391.1 5.4 slice-start.1
  410.2 5.8 copy-start.46
  415.9 157.3 %reduce-scatter.2.cloned.1.call-start = ((), (), s32[]{:S(2)}) async-start(), calls=%async_computation.3 | async-start | bytes 3276800 | tf_op jit(solution)/shard_map/reduce_scatter | solution.py:104
  427.1 7.3 %copy-start.25 = (f32[1280]{0:T(1024)S(1)}, f32[1280]{0:T(1024)}, u32[]{:S(2)}) copy-start(f32[1280]{0:T(1024)} %copy-done.23) | copy-start | bytes 15364
  427.1 7.3 %copy-start.31 = (f32[1280]{0:T(1024)S(1)}, f32[1280]{0:T(1024)}, u32[]{:S(2)}) copy-start(f32[1280]{0:T(1024)} %copy-done.29) | copy-start | bytes 15364
  427.1 7.3 %copy-start.38 = (f32[1024]{0:T(1024)S(1)}, f32[1024]{0:T(1024)}, u32[]{:S(2)}) copy-start(f32[1024]{0:T(1024)} %param.24) | copy-start | bytes 12292
  427.2 7.3 %copy-start.50 = (f32[1024]{0:T(1024)S(1)}, f32[1024]{0:T(1024)}, u32[]{:S(2)}) copy-start(f32[1024]{0:T(1024)} %param.25) | copy-start | bytes 12292
  427.2 254.4 %all-reduce.13.cloned.1.call-start = ((), (), s32[]{:S(2)}) async-start(), calls=%async_computation.7 | async-start | bytes 12582912 | tf_op jit(solution)/shard_map/psum | solution.py:169
  427.4 7.1 %copy-start.52 = (bf16[1280,1024]{1,0:T(8,128)(2,1)S(1)}, bf16[1280,1024]{1,0:T(8,128)(2,1)}, u32[]{:S(2)}) copy-start(bf16[1280,1024]{1,0:T(8,128)(2,1)} %copy-done.51) | copy-start | bytes 7864324
  427.4 14.4 %slice-start.2 = ((s8[5242880]{0:T(1024)(128)(4,1)}), s8[4194304]{0:T(1024)(128)(4,1)S(1)}, s32[]{:S(2)}) async-start(s8[5242880]{0:T(1024)(128)(4,1)} %bitcast.97), calls=%async_computation.10 | async-start | bytes 8388608
  434.5 7.3 %slice-start.3 = ((s8[5242880]{0:T(1024)(128)(4,1)}), s8[1048576]{0:T(1024)(128)(4,1)S(1)}, s32[]{:S(2)}) async-start(s8[5242880]{0:T(1024)(128)(4,1)} %bitcast.97), calls=%async_computation.11 | async-start | bytes 2097152
  447.8 73.6 %copy-start.40 = (f32[1024]{0:T(1024)S(1)}, f32[1024]{0:T(1024)}, u32[]{:S(2)}) copy-start(f32[1024]{0:T(1024)} %param.18) | copy-start | bytes 12292
  521.4 7.5 %copy-start.41 = (bf16[1024]{0:T(1024)(128)(2,1)S(1)}, bf16[1024]{0:T(1024)(128)(2,1)}, u32[]{:S(2)}) copy-start(bf16[1024]{0:T(1024)(128)(2,1)} %get-tuple-element.35) | copy-start | bytes 6148
  521.4 7.5 %copy-start.42 = (bf16[1024]{0:T(1024)(128)(2,1)S(1)}, bf16[1024]{0:T(1024)(128)(2,1)}, u32[]{:S(2)}) copy-start(bf16[1024]{0:T(1024)(128)(2,1)} %get-tuple-element.46) | copy-start | bytes 6148
  521.4 7.5 %copy-start.43 = (bf16[1024]{0:T(1024)(128)(2,1)S(1)}, bf16[1024]{0:T(1024)(128)(2,1)}, u32[]{:S(2)}) copy-start(bf16[1024]{0:T(1024)(128)(2,1)} %get-tuple-element.14) | copy-start | bytes 6148
  521.4 7.5 %copy-start.47 = (bf16[1024]{0:T(1024)(128)(2,1)S(1)}, bf16[1024]{0:T(1024)(128)(2,1)}, u32[]{:S(2)}) copy-start(bf16[1024]{0:T(1024)(128)(2,1)} %get-tuple-element.32) | copy-start | bytes 6148
  681.6 5.8 copy-start.17
  683.9 6.0 copy-start.16
  (16 other events, 30.0 us)
Sparse Core Ops, SparseCore 0:
  9.6 57.5 all-gather.2
  68.7 52.9 all-gather.4
  124.7 102.2 all-reduce.6
  261.0 103.0 all-reduce.8
  416.1 103.0 all-reduce.10
  521.9 51.2 reduce-scatter.1
  578.0 103.5 all-reduce.12
where the time goes:
time: 709 us; the launch traced here: 699 us
  waiting for transfers between devices  459 us (65%)
  matrix products  80.7 us (11%)
  other arithmetic  67.8 us (10%)
  local copies, waits for them, and re-layouts  51.3 us (7%)
  blocking collectives  24.7 us (3%)
  between operations  15.1 us (2%)
    psum x1, waiting for transfers between devices, per_device(): lax.psum(attn_part.astype(jnp.bfloat16), 'tensor').astype(jnp.float32)  105 us
    psum x1, waiting for transfers between devices, per_device(): lax.psum(grad_w_qkv.astype(jnp.bfloat16), 'dp').astype(jnp.float32)  104 us
    psum x1, waiting for transfers between devices, per_device(): lax.psum(hidden_part.astype(jnp.bfloat16), 'tensor').astype(jnp.float32)  102 us
    psum x1, waiting for transfers between devices, per_device(): lax.psum(normed_part.astype(jnp.bfloat16), 'tensor').astype(jnp.float32)  67.9 us
    all_gather x1, waiting for transfers between devices, per_device(): lax.all_gather(images, 'tensor', axis=2, tiled=True)  54.3 us
    psum x1, blocking collectives, per_device(): lax.psum(grad_norm1_gain.astype(jnp.bfloat16), 'dp').astype(jnp.float32)  24.7 us
    unnamed x118, local copies, waits for them, and re-layouts  20.9 us
    dot_general x1, matrix products, per_device(): jnp.einsum('rd,fd->rf', grad_ff, w_fc2, preferred_element_type=jnp.float32)  16.8 us
  transfers between devices with their start and end apart: 7, of which 7 were waited for; matrix products, arithmetic and copies ran while one was open for 14% of the time, Pallas kernels for 0%

commit v1 on v0

--- a/solution.py
+++ b/solution.py
@@ -2,6 +2,7 @@
 import jax.numpy as jnp
 from jax import lax
 from jax.sharding import PartitionSpec as P
+from jax.lax import all_gather
 
 HEAD_DIM = 64
 EPS = 1e-06
@@ -93,7 +94,7 @@
     attn_part = jnp.dot(mixed_rows, w_proj, preferred_element_type=jnp.float32)
     middle = (
         row_values
-        + lax.psum(attn_part.astype(jnp.bfloat16), "tensor").astype(jnp.float32)
+        + all_gather(attn_part.astype(jnp.bfloat16), "tensor").sum(axis=0).astype(jnp.float32)
         + proj_bias
     )
     normed2, unit2, inverse2 = norm_rows(middle, norm2_gain, norm2_shift)

time: 709 us -> 827 us (1.17)
  waiting for transfers between devices: 459 us -> 558 us
  other arithmetic: 67.8 us -> 87.2 us
    all_gather x0 -> x1, waiting for transfers between devices: none -> 181 us  [per_device(): all_gather(attn_part.astype(jnp.bfloat16), 'tensor').sum(axis=0)]
    psum x1 -> x0, waiting for transfers between devices: 105 us -> none  [per_device(): lax.psum(attn_part.astype(jnp.bfloat16), 'tensor').astype(jnp.float32)]
    all_gather x1, waiting for transfers between devices: 9.45 us -> 31.4 us  [per_device(): lax.all_gather(cotangent, 'tensor', axis=2, tiled=True)]
    reduce_sum x0 -> x1, other arithmetic: none -> 8.97 us  [per_device(): all_gather(attn_part.astype(jnp.bfloat16), 'tensor').sum(axis=0)]
  transfers between devices with their start and end apart: 7 -> 7, of which waited for: 7 -> 7; matrix products, arithmetic and copies ran while one was open for 14% -> 10% of each run, Pallas kernels for 0% -> 0%
where the time goes in v1:
time: 827 us; the launch traced here: 817 us
  waiting for transfers between devices  558 us (67%)
  other arithmetic  87.2 us (11%)
  matrix products  80.7 us (10%)
  local copies, waits for them, and re-layouts  51.7 us (6%)
  blocking collectives  24.7 us (3%)
  between operations  15.1 us (2%)
    all_gather x1, waiting for transfers between devices, per_device(): all_gather(attn_part.astype(jnp.bfloat16), 'tensor').sum(axis=0)  181 us
    psum x1, waiting for transfers between devices, per_device(): lax.psum(grad_w_qkv.astype(jnp.bfloat16), 'dp').astype(jnp.float32)  104 us
    psum x1, waiting for transfers between devices, per_device(): lax.psum(hidden_part.astype(jnp.bfloat16), 'tensor').astype(jnp.float32)  101 us
    psum x1, waiting for transfers between devices, per_device(): lax.psum(normed_part.astype(jnp.bfloat16), 'tensor').astype(jnp.float32)  68 us
    all_gather x1, waiting for transfers between devices, per_device(): lax.all_gather(images, 'tensor', axis=2, tiled=True)  55.1 us
    all_gather x1, waiting for transfers between devices, per_device(): lax.all_gather(cotangent, 'tensor', axis=2, tiled=True)  31.4 us
    psum x1, blocking collectives, per_device(): lax.psum(grad_norm1_gain.astype(jnp.bfloat16), 'dp').astype(jnp.float32)  24.7 us
    unnamed x118, local copies, waits for them, and re-layouts  18.5 us
  transfers between devices with their start and end apart: 7, of which 7 were waited for; matrix products, arithmetic and copies ran while one was open for 10% of the time, Pallas kernels for 0%

profile of v1, /device:TPU:0, one launch (start us, length us, event | category | flops | bytes accessed | tf_op | source)
XLA Modules:
  0.0 817.4 jit_solution(1606800124437384962)
XLA Ops:
  8.0 2.6 copy.39
  12.1 55.1 %all-gather.5.cloned.1.call-done = bf16[4,320,1024]{2,1,0:T(8,128)(2,1)} async-done(((bf16[4,320,256]{2,1,0:T(8,128)(2,1)}), bf16[4,320,1024]{2,1,0:T(8,128)(2,1)}) %all-gather.5.cloned.1.call-update) | async-done | bytes 2621456 | tf_op jit(solution)/shard_map/all_gather | solution.py:65
  67.2 2.6 fusion.18
  69.8 2.8 multiply_reduce_fusion.3
  75.4 3.5 add_convert_fusion.3
  78.9 6.7 reshape.309
  85.6 3.9 fusion.57
  91.8 2.5 copy.65
  94.3 3.2 copy.66
  97.5 3.2 fusion.24
  102.7 2.4 fusion.36
  108.7 3.4 convolution_convert_fusion.1
  113.0 181.4 %all-gather.9.cloned.1.call-done = bf16[5120,1024]{1,0:T(8,128)(2,1)} async-done(((bf16[1280,1024]{1,0:T(8,128)(2,1)}), bf16[5120,1024]{1,0:T(8,128)(2,1)}) %all-gather.9.cloned.1.call-update) | async-done | bytes 10485776 | tf_op jit(solution)/shard_map/all_gather | solution.py:97
  294.3 9.0 %reduce_sum.192 = bf16[1280,1024]{1,0:T(8,128)(2,1)} reduce(bf16[4,1280,1024]{2,1,0:T(8,128)(2,1)} %bitcast.102, bf16[]{:T(256)} %constant.17.clone.1), dimensions={0}, to_apply=%region_4.5 | reduce | flops 3932160 | bytes 13107202 | tf_op jit(solution)/shard_map/reduce_sum | solution.py:97
  303.3 6.2 fusion.25
  311.5 4.1 multiply_reduce_fusion.2
  317.6 31.4 %all-gather.7.cloned.1.call-done = bf16[4,320,1024]{2,1,0:T(8,128)(2,1)} async-done(((bf16[4,320,256]{2,1,0:T(8,128)(2,1)}), bf16[4,320,1024]{2,1,0:T(8,128)(2,1)}) %all-gather.7.cloned.1.call-update) | async-done | bytes 2621456 | tf_op jit(solution)/shard_map/all_gather | solution.py:66
  349.0 4.8 add_add_fusion.1
  353.9 3.1 fusion.52
  357.0 16.8 %fusion.53 = (bf16[1024]{0:T(1024)(128)(2,1)}, bf16[1280,1024]{1,0:T(8,128)(2,1)S(1)}, f32[1280,1024]{1,0:T(8,128)}) fusion(f32[1280,1024]{1,0:T(8,128)S(1)} %fusion.52, f32[1024]{0:T(1024)S(1)} %copy-done.45, bf16[1280,1024]{1,0:T(8,128)(2,1)S(1)} %get-tuple-element.50, bf16[1024,1024]{1,0:T(8,128)(2,1)S(1)} %copy-done), kind=kOutput, calls=%fused_computation.115 | convolution fusion | flops 2781346816 | bytes 17831936 | tf_op jit(solution)/shard_map/rd,fd->rf/dot_general | solution.py:116
  375.4 4.2 convolution_convert_fusion.2
  381.1 101.0 %all-reduce.6.cloned.1.call-done = bf16[1280,1024]{1,0:T(8,128)(2,1)} async-done(((bf16[1280,1024]{1,0:T(8,128)(2,1)}), bf16[1280,1024]{1,0:T(8,128)(2,1)}) %all-reduce.6.cloned.1.call-update) | async-done | bytes 2621456 | tf_op jit(solution)/shard_map/psum | solution.py:122
  482.1 5.5 fusion.9
  487.6 5.6 convert_reduce_fusion
  493.2 2.3 copy-done.4
  497.2 3.1 reshape.310
  500.3 3.2 copy.47
  503.6 5.5 fusion.28
  509.2 5.4 multiply_reduce_fusion
  514.6 2.9 multiply_convert_fusion
  520.3 3.2 copy.52
  523.5 4.7 convert_element_type.239
  528.3 5.7 convolution_convert_fusion
  534.1 5.5 multiply_convert_fusion.2
  541.0 4.1 convolution_convert_fusion.3
  545.4 7.0 convolution_convert_fusion.5
  552.5 7.3 convolution_convert_fusion.6
  562.4 3.4 convolution_convert_fusion.7
  566.8 2.3 fusion.26
  569.3 68.0 %all-reduce.8.cloned.1.call-done = bf16[1280,1024]{1,0:T(8,128)(2,1)} async-done(((bf16[1280,1024]{1,0:T(8,128)(2,1)}), bf16[1280,1024]{1,0:T(8,128)(2,1)}) %all-reduce.8.cloned.1.call-update) | async-done | bytes 2621456 | tf_op jit(solution)/shard_map/psum | solution.py:161
  639.5 7.2 fusion.10
  646.7 24.7 %all-reduce = (bf16[1024]{0:T(1024)(128)(2,1)S(1)}, bf16[1024]{0:T(1024)(128)(2,1)S(1)}, bf16[2,256]{1,0:T(2,128)(2,1)S(1)}, bf16[1024]{0:T(1024)(128)(2,1)S(1)}...) all-reduce(bf16[1024]{0:T(1024)(128)(2,1)S(1)} %get-tuple-element.1, ...), channel_id=1, replica_groups=mesh['dp'=8,'tensor'=4] {'dp'}, use_global_device_ids=true, to_apply=%region_16.17 | all-reduce | flops 7680 | bytes 30720 | tf_op jit(solution)/shard_map/psum | solution.py:168
  676.2 15.1 %reduce-scatter.2.cloned.1.call-done = bf16[1280,256]{1,0:T(8,128)(2,1)} async-done(((bf16[1280,1024]{1,0:T(8,128)(2,1)}), bf16[1280,256]{1,0:T(8,128)(2,1)}) %reduce-scatter.2.cloned.1.call-update) | async-done | bytes 655376 | tf_op jit(solution)/shard_map/reduce_scatter | solution.py:105
  691.3 4.1 fusion.33
  695.4 104.3 %all-reduce.10.cloned.1.call-done = (bf16[1024,3,256]{2,0,1:T(8,128)(2,1)}, bf16[256,1024]{1,0:T(8,128)(2,1)}, bf16[1024,1024]{1,0:T(8,128)(2,1)}, bf16[1024,1024]{1,0:T(8,128)(2,1)}) async-done(((bf16[1024,3,256]{2,0,1:T(8,128)(2,1)}, bf16[256,1024]{1,0:T(8,128)(2,1)}, bf16[1024,1024]{1,0:T(8,128)(2,1)}, bf16[1024,1024]{1,0:T(8,128)(2,1)}), (bf16[1024,3,256]{2,0,1:T(8,128)(2,1)}, ...) | async-done | bytes 6291472 | tf_op jit(solution)/shard_map/psum | solution.py:170
  801.9 3.5 convert_element_type.247
  805.4 2.5 convert_element_type.257
  807.9 2.5 convert_element_type.260
  (171 shorter events, 40.0 us)
Async XLA Ops:
  7.2 349.8 %copy-start = (bf16[1024,1024]{1,0:T(8,128)(2,1)S(1)}, bf16[1024,1024]{1,0:T(8,128)(2,1)}, u32[]{:S(2)}) copy-start(bf16[1024,1024]{1,0:T(8,128)(2,1)} %param.28) | copy-start | bytes 6291460
  7.2 65.3 %copy-start.39 = (f32[1024]{0:T(1024)S(1)}, f32[1024]{0:T(1024)}, u32[]{:S(2)}) copy-start(f32[1024]{0:T(1024)} %param.18) | copy-start | bytes 12292
  7.2 65.3 %copy-start.44 = (f32[1024]{0:T(1024)S(1)}, f32[1024]{0:T(1024)}, u32[]{:S(2)}) copy-start(f32[1024]{0:T(1024)} %param.19) | copy-start | bytes 12292
  7.2 60.0 %all-gather.5.cloned.1.call-start = ((), (), s32[]{:S(2)}) async-start(), calls=%async_computation.1 | async-start | bytes 3276800 | tf_op jit(solution)/shard_map/all_gather | solution.py:65
  8.0 286.4 %all-gather.9.cloned.1.call-start = ((), (), s32[]{:S(2)}) async-start(), calls=%async_computation.6 | async-start | bytes 13107200 | tf_op jit(solution)/shard_map/all_gather | solution.py:97
  12.1 90.6 %copy-start.34 = (pred[4,320]{1,0:T(4,128)(4,1)}, pred[4,320]{1,0:T(4,128)(4,1)S(1)}, u32[]{:S(2)}) copy-start(pred[4,320]{1,0:T(4,128)(4,1)S(1)} %get-tuple-element.55) | copy-start | bytes 3844
  67.2 5.4 copy-start.1
  67.2 8.2 %copy-start.20 = (bf16[1024,3,256]{0,2,1:T(8,128)(2,1)S(1)}, bf16[1024,3,256]{0,2,1:T(8,128)(2,1)}, u32[]{:S(2)}) copy-start(bf16[1024,3,256]{0,2,1:T(8,128)(2,1)} %copy.39) | copy-start | bytes 4718596
  100.7 4.4 copy-start.2
  100.7 4.4 copy-start.22
  112.1 236.8 %all-gather.7.cloned.1.call-start = ((), (), s32[]{:S(2)}) async-start(), calls=%async_computation.3 | async-start | bytes 3276800 | tf_op jit(solution)/shard_map/all_gather | solution.py:66
  112.9 369.2 %all-reduce.6.cloned.1.call-start = ((), (), s32[]{:S(2)}) async-start(), calls=%async_computation.4 | async-start | bytes 5242880 | tf_op jit(solution)/shard_map/psum | solution.py:122
  349.0 4.9 copy-start.26
  349.0 4.9 copy-start.29
  349.0 4.9 copy-start.36
  349.0 4.9 copy-start.48
  349.0 4.9 copy-start.49
  357.0 16.9 %copy-start.8 = (f32[1280,1024]{1,0:T(8,128)}, f32[1280,1024]{1,0:T(8,128)S(1)}, u32[]{:S(2)}) copy-start(f32[1280,1024]{1,0:T(8,128)S(1)} %fusion.52) | copy-start | bytes 15728644
  379.7 257.6 %all-reduce.8.cloned.1.call-start = ((), (), s32[]{:S(2)}) async-start(), calls=%async_computation.5 | async-start | bytes 5242880 | tf_op jit(solution)/shard_map/psum | solution.py:161
  482.1 5.5 copy-start.5
  482.1 5.5 copy-start.6
  482.1 5.5 copy-start.27
  482.1 5.5 copy-start.30
  482.1 5.5 copy-start.37
  487.6 7.9 copy-start.18
  503.6 5.5 copy-start.10
  503.6 5.6 copy-start.11
  503.6 5.6 copy-start.21
  503.6 5.6 copy-start.35
  503.6 11.0 %slice-start = ((s8[7864320]{0:T(1024)(128)(4,1)}), s8[4194304]{0:T(1024)(128)(4,1)S(1)}, s32[]{:S(2)}) async-start(s8[7864320]{0:T(1024)(128)(4,1)} %bitcast.97), calls=%async_computation.8 | async-start | bytes 8388608
  509.2 5.4 slice-start.1
  528.2 5.8 copy-start.46
  534.0 157.3 %reduce-scatter.2.cloned.1.call-start = ((), (), s32[]{:S(2)}) async-start(), calls=%async_computation.2 | async-start | bytes 3276800 | tf_op jit(solution)/shard_map/reduce_scatter | solution.py:105
  545.2 7.3 copy-start.28
  545.2 7.3 copy-start.31
  545.2 7.3 copy-start.38
  545.2 7.3 copy-start.50
  545.2 254.5 %all-reduce.10.cloned.1.call-start = ((), (), s32[]{:S(2)}) async-start(), calls=%async_computation.7 | async-start | bytes 12582912 | tf_op jit(solution)/shard_map/psum | solution.py:170
  545.4 7.1 copy-start.52
  545.4 14.4 %slice-start.2 = ((s8[5242880]{0:T(1024)(128)(4,1)}), s8[4194304]{0:T(1024)(128)(4,1)S(1)}, s32[]{:S(2)}) async-start(s8[5242880]{0:T(1024)(128)(4,1)} %bitcast.99), calls=%async_computation.10 | async-start | bytes 8388608
  552.5 7.3 slice-start.3
  565.8 73.7 %copy-start.40 = (f32[1024]{0:T(1024)S(1)}, f32[1024]{0:T(1024)}, u32[]{:S(2)}) copy-start(f32[1024]{0:T(1024)} %param.18) | copy-start | bytes 12292
  639.5 7.3 copy-start.41
  639.5 7.2 copy-start.42
  639.5 7.2 copy-start.43
  639.5 7.2 copy-start.47
  799.7 5.8 copy-start.17
  801.9 6.0 copy-start.16
  (16 other events, 33.8 us)
Sparse Core Ops, SparseCore 0:
  9.6 57.5 all-gather.4
  112.2 182.0 all-gather.8
  295.9 52.9 all-gather.6
  379.8 102.2 all-reduce.5
  534.1 103.0 all-reduce.7
  640.0 51.2 reduce-scatter.1
  696.1 103.5 all-reduce.9
